TPU v7x, 32 devices: a whole 2x2x4 slice. The times are simulated.
32 devices in a mesh: rep: 2 (over y), shard: 16 (over z, x, core).
Axes of the slice: x: 2, y: 2, z: 4, core: 2. Of those that a mesh axis runs over, the one named last changes fastest.
Arguments:
- tokens: bfloat16 [2, 3072, 768], P('rep', 'shard'), may hold values from -6 to 6
- segments: int32 [2, 3072], P('rep', 'shard'), may hold values from 0 to 16, never falling along the last dimension, each value on 1 to 2304 neighbouring positions
- padding: int32 [2, 3072], P('rep', 'shard'), may hold values from 0 to 1, as said below
- query_weight: float32 [768, 768], P('shard'), may hold values from -0.21875 to 0.21875
- key_weight: float32 [768, 768], P('shard'), may hold values from -0.21875 to 0.21875
- value_weight: float32 [768, 768], P('shard'), may hold values from -0.21875 to 0.21875
- query_bias: float32 [768], P('shard'), may hold values from -3 to 3
- value_bias: float32 [768], P('shard'), may hold values from -3 to 3
- out_weight: float32 [768, 768], P('shard'), may hold values from -0.875 to 0.875
- out_bias: float32 [768], P('shard'), may hold values from -3 to 3
- middle_gain: float32 [768], P('shard'), may hold values from 0.5 to 1.5
- middle_shift: float32 [768], P('shard'), may hold values from -3 to 3
- up_weight: float32 [768, 3072], P('shard'), may hold values from -0.21875 to 0.21875
- up_bias: float32 [3072], P('shard'), may hold values from -3 to 3
- down_weight: float32 [3072, 768], P('shard'), may hold values from -0.109375 to 0.109375
- down_bias: float32 [768], P('shard'), may hold values from -3 to 3
- final_gain: float32 [768], P('shard'), may hold values from 0.5 to 1.5
- final_shift: float32 [768], P('shard'), may hold values from -3 to 3
- cotangent: bfloat16 [2, 3072, 768], P('rep', 'shard'), may hold values from -6 to 6
Outputs:
- output: bfloat16 [2, 3072, 768], P('rep', 'shard')
- grad_tokens: bfloat16 [2, 3072, 768], P('rep', 'shard')
- grad_query_weight: float32 [768, 768], P('shard')
- grad_key_weight: float32 [768, 768], P('shard')
- grad_value_weight: float32 [768, 768], P('shard')
- grad_query_bias: float32 [768], P('shard')
- grad_value_bias: float32 [768], P('shard')
- grad_out_weight: float32 [768, 768], P('shard')
- grad_out_bias: float32 [768], P('shard')
- grad_middle_gain: float32 [768], P('shard')
- grad_middle_shift: float32 [768], P('shard')
- grad_up_weight: float32 [768, 3072], P('shard')
- grad_up_bias: float32 [3072], P('shard')
- grad_down_weight: float32 [3072, 768], P('shard')
- grad_down_bias: float32 [768], P('shard')
- grad_final_gain: float32 [768], P('shard')
- grad_final_shift: float32 [768], P('shard')
Inputs may be any that keep to these rules, and one draw needn't show every extreme that they name: `segments`: within each sequence the numbers never fall; every document has 1 to 2304 tokens and one has exactly 2304. Each sequence ends with a run of at least one padding token and has no other padding.
All inputs are finite; a program needn't handle non-finite values.
Results may differ from a plain program's by a relative error of at most 0.024.
Values may be sent and summed in bfloat16 or wider, within the bound.
A program may use at most 256 MiB of HBM per device.

v0:
```python
import jax
import jax.numpy as jnp
from jax import lax
from jax.sharding import PartitionSpec as P

D = 768
HEADS = 12
HEAD_DIM = 64
epsilon = 1e-12
very_low = -1e30
block_size = 512
root_half = 0.7071067811865476
inv_root_tau = 0.3989422804014327


def split_size():
    return block_size


def over_blocks(update, initial, arrays, total_rows):
    length = split_size()
    number = total_rows // length
    split = tuple((item.reshape((number, length) + item.shape[1:]) for item in arrays))

    def advance(carried, pieces):
        return (update(carried, pieces), None)

    return lax.scan(advance, initial, split)[0]


def scan_blocks(step, initial, arrays, total_rows):
    length = split_size()
    number = total_rows // length
    split = tuple((item.reshape((number, length) + item.shape[1:]) for item in arrays))
    final, produced = lax.scan(step, initial, split)
    return (final, produced.reshape((total_rows,) + produced.shape[2:]))


def guarded_update(update):

    def run_update(carried, pieces):
        return update(carried, pieces)

    return run_update


def guarded_step(step):

    def run_step(carried, pieces):
        return step(carried, pieces)

    return run_step


def norm_forward(value, gain, shift):
    center = value - jnp.mean(value, axis=-1, keepdims=True)
    spread = jnp.mean(center * center, axis=-1, keepdims=True)
    scale = lax.rsqrt(spread + epsilon)
    normal = center * scale
    return (normal * gain + shift, normal, scale)


def norm_backward(upstream, normal, scale, gain):
    inner = upstream * gain
    return scale * (
        inner
        - jnp.mean(inner, axis=-1, keepdims=True)
        - normal * jnp.mean(inner * normal, axis=-1, keepdims=True)
    )


def gelu_slope(hidden):
    return 0.5 * (1.0 + lax.erf(hidden * root_half)) + hidden * inv_root_tau * jnp.exp(
        -0.5 * hidden * hidden
    )


def score_grads(
    queries, query_codes, log_rows, delta_rows, dctx_rows, key_rows, value_rows, key_codes
):
    raw_scores = (
        jnp.einsum("qhd,khd->hqk", queries, key_rows, preferred_element_type=jnp.float32) * 0.125
    )
    allowed = (query_codes[:, None] == key_codes[None, :])[None]
    chances = jnp.where(allowed, jnp.exp(raw_scores - log_rows[:, :, None]), 0.0)
    d_chance = jnp.einsum("qhd,khd->hqk", dctx_rows, value_rows, preferred_element_type=jnp.float32)
    d_score = (chances * (d_chance - delta_rows[:, :, None])).astype(jnp.bfloat16)
    return (chances, d_score)


def forward_update(queries, codes_here):

    def update(carried, pieces):
        running_top, running_total, context_sum = carried
        key_rows, value_rows, key_codes = pieces
        raw_scores = (
            jnp.einsum("qhd,khd->hqk", queries, key_rows, preferred_element_type=jnp.float32)
            * 0.125
        )
        allowed = (codes_here[:, None] == key_codes[None, :])[None]
        masked = jnp.where(allowed, raw_scores, very_low)
        new_top = jnp.maximum(running_top, jnp.max(masked, axis=2))
        rescale = jnp.exp(running_top - new_top)
        weights = jnp.where(allowed, jnp.exp(masked - new_top[:, :, None]), 0.0)
        new_total = running_total * rescale + jnp.sum(weights, axis=2)
        added = jnp.einsum(
            "hqk,khd->qhd",
            weights.astype(jnp.bfloat16),
            value_rows,
            preferred_element_type=jnp.float32,
        )
        return (new_top, new_total, context_sum * rescale.T[:, :, None] + added)

    return guarded_update(update)


def shards(
    tokens,
    segments,
    padding,
    query_weight,
    key_weight,
    value_weight,
    query_bias,
    value_bias,
    out_weight,
    out_bias,
    middle_gain,
    middle_shift,
    up_weight,
    up_bias,
    down_weight,
    down_bias,
    final_gain,
    final_shift,
    cotangent,
):
    w_query, w_key, w_value, w_out, b_query, b_value, b_out, gain_mid, shift_mid = (
        lax.all_gather(query_weight.astype(jnp.bfloat16), "shard", axis=0, tiled=True),
        lax.all_gather(key_weight.astype(jnp.bfloat16), "shard", axis=0, tiled=True),
        lax.all_gather(value_weight.astype(jnp.bfloat16), "shard", axis=0, tiled=True),
        lax.all_gather(out_weight.astype(jnp.bfloat16), "shard", axis=0, tiled=True),
        lax.all_gather(query_bias.astype(jnp.bfloat16), "shard", axis=0, tiled=True),
        lax.all_gather(value_bias.astype(jnp.bfloat16), "shard", axis=0, tiled=True),
        lax.all_gather(out_bias.astype(jnp.bfloat16), "shard", axis=0, tiled=True),
        lax.all_gather(middle_gain.astype(jnp.bfloat16), "shard", axis=0, tiled=True),
        lax.all_gather(middle_shift.astype(jnp.bfloat16), "shard", axis=0, tiled=True),
    )
    w_up, b_up, w_down, b_down, gain_end, shift_end = (
        lax.all_gather(up_weight.astype(jnp.bfloat16), "shard", axis=0, tiled=True),
        lax.all_gather(up_bias.astype(jnp.bfloat16), "shard", axis=0, tiled=True),
        lax.all_gather(down_weight.astype(jnp.bfloat16), "shard", axis=0, tiled=True),
        lax.all_gather(down_bias.astype(jnp.bfloat16), "shard", axis=0, tiled=True),
        lax.all_gather(final_gain.astype(jnp.bfloat16), "shard", axis=0, tiled=True),
        lax.all_gather(final_shift.astype(jnp.bfloat16), "shard", axis=0, tiled=True),
    )
    own_tokens = tokens[0]
    here_rows = own_tokens.shape[0]
    own_codes = 2 * segments[0] + padding[0]
    all_codes = lax.all_gather(own_codes, "shard", axis=0, tiled=True)
    queries_flat = (
        jnp.dot(own_tokens, w_query, preferred_element_type=jnp.float32)
        + b_query.astype(jnp.float32)
    ).astype(jnp.bfloat16)
    keys_flat = jnp.dot(own_tokens, w_key, preferred_element_type=jnp.float32).astype(jnp.bfloat16)
    values_flat = (
        jnp.dot(own_tokens, w_value, preferred_element_type=jnp.float32)
        + b_value.astype(jnp.float32)
    ).astype(jnp.bfloat16)
    keys_all, values_all = (
        lax.all_gather(keys_flat, "shard", axis=0, tiled=True),
        lax.all_gather(values_flat, "shard", axis=0, tiled=True),
    )
    seq_rows = keys_all.shape[0]
    queries = queries_flat.reshape(here_rows, HEADS, HEAD_DIM)
    key_heads = keys_all.reshape(seq_rows, HEADS, HEAD_DIM)
    value_heads = values_all.reshape(seq_rows, HEADS, HEAD_DIM)
    start_state = (
        jnp.full((HEADS, here_rows), very_low, jnp.float32),
        jnp.zeros((HEADS, here_rows), jnp.float32),
        jnp.zeros((here_rows, HEADS, HEAD_DIM), jnp.float32),
    )
    best_score, total_weight, context_sum = over_blocks(
        forward_update(queries, own_codes),
        start_state,
        (key_heads, value_heads, all_codes),
        seq_rows,
    )
    log_total = best_score + jnp.log(total_weight)
    context = (context_sum / total_weight.T[:, :, None]).reshape(here_rows, D)
    context_low = context.astype(jnp.bfloat16)
    branch = jnp.dot(context_low, w_out, preferred_element_type=jnp.float32) + b_out.astype(
        jnp.float32
    )
    middle, normal_mid, scale_mid = norm_forward(
        own_tokens.astype(jnp.float32) + branch,
        gain_mid.astype(jnp.float32),
        shift_mid.astype(jnp.float32),
    )
    middle_low = middle.astype(jnp.bfloat16)
    hidden = jnp.dot(middle_low, w_up, preferred_element_type=jnp.float32) + b_up.astype(
        jnp.float32
    )
    active_low = jax.nn.gelu(hidden, approximate=False).astype(jnp.bfloat16)
    feed = jnp.dot(active_low, w_down, preferred_element_type=jnp.float32) + b_down.astype(
        jnp.float32
    )
    result, normal_end, scale_end = norm_forward(
        middle + feed, gain_end.astype(jnp.float32), shift_end.astype(jnp.float32)
    )
    output = result.astype(jnp.bfloat16)[None]
    upstream = cotangent[0].astype(jnp.float32)
    grad_gain_end = jnp.sum(upstream * normal_end, axis=0)
    grad_shift_end = jnp.sum(upstream, axis=0)
    d_second = norm_backward(upstream, normal_end, scale_end, gain_end.astype(jnp.float32))
    feed_low = d_second.astype(jnp.bfloat16)
    grad_down = lax.psum_scatter(
        jnp.einsum("tf,td->fd", active_low, feed_low, preferred_element_type=jnp.float32).astype(
            jnp.bfloat16
        ),
        "shard",
        scatter_dimension=0,
        tiled=True,
    )
    d_active = jnp.einsum("td,fd->tf", feed_low, w_down, preferred_element_type=jnp.float32)
    up_low = (d_active * gelu_slope(hidden)).astype(jnp.bfloat16)
    grad_up = lax.psum_scatter(
        jnp.einsum("td,tf->df", middle_low, up_low, preferred_element_type=jnp.float32).astype(
            jnp.bfloat16
        ),
        "shard",
        scatter_dimension=0,
        tiled=True,
    )
    d_middle = jnp.einsum("tf,df->td", up_low, w_up, preferred_element_type=jnp.float32) + d_second
    grad_gain_mid = jnp.sum(d_middle * normal_mid, axis=0)
    grad_shift_mid = jnp.sum(d_middle, axis=0)
    d_first = norm_backward(d_middle, normal_mid, scale_mid, gain_mid.astype(jnp.float32))
    branch_low = d_first.astype(jnp.bfloat16)
    dctx_low = jnp.einsum(
        "te,de->td", branch_low, w_out, preferred_element_type=jnp.float32
    ).astype(jnp.bfloat16)
    dctx_heads = dctx_low.reshape(here_rows, HEADS, HEAD_DIM)
    delta = jnp.sum(
        dctx_heads.astype(jnp.float32) * context.reshape(here_rows, HEADS, HEAD_DIM), axis=2
    ).T
    empty_heads = jnp.zeros((here_rows, HEADS, HEAD_DIM), jnp.float32)

    def key_step(carried, pieces):
        key_rows, value_rows, key_codes = pieces
        chances, d_score = score_grads(
            queries, own_codes, log_total, delta, dctx_heads, key_rows, value_rows, key_codes
        )
        block_rows = key_rows.shape[0]
        query_part = (
            carried
            + jnp.einsum("hqk,khd->qhd", d_score, key_rows, preferred_element_type=jnp.float32)
            * 0.125
        )
        d_key = (
            jnp.einsum("hqk,qhd->khd", d_score, queries, preferred_element_type=jnp.float32) * 0.125
        )
        d_value = jnp.einsum(
            "hqk,qhd->khd",
            chances.astype(jnp.bfloat16),
            dctx_heads,
            preferred_element_type=jnp.float32,
        )
        return (
            query_part,
            jnp.concatenate([d_key.reshape(block_rows, D), d_value.reshape(block_rows, D)], axis=1),
        )

    d_query, key_value_terms = scan_blocks(
        guarded_step(key_step), empty_heads, (key_heads, value_heads, all_codes), seq_rows
    )
    summed_kv = lax.psum_scatter(
        key_value_terms.astype(jnp.bfloat16), "shard", scatter_dimension=0, tiled=True
    ).astype(jnp.float32)
    key_grad = summed_kv[:, :D]
    value_grad = summed_kv[:, D:]
    query_low = d_query.reshape(here_rows, D).astype(jnp.bfloat16)
    key_low = key_grad.astype(jnp.bfloat16)
    value_low = value_grad.astype(jnp.bfloat16)
    mixer_part = lax.psum_scatter(
        jnp.concatenate(
            [
                jnp.einsum("td,te->de", own_tokens, query_low, preferred_element_type=jnp.float32),
                jnp.einsum("td,te->de", own_tokens, key_low, preferred_element_type=jnp.float32),
                jnp.einsum("td,te->de", own_tokens, value_low, preferred_element_type=jnp.float32),
                jnp.einsum(
                    "td,te->de", context_low, branch_low, preferred_element_type=jnp.float32
                ),
            ],
            axis=1,
        ).astype(jnp.bfloat16),
        "shard",
        scatter_dimension=0,
        tiled=True,
    )
    grad_input = jnp.einsum("te,de->td", query_low, w_query, preferred_element_type=jnp.float32)
    grad_input = grad_input + jnp.einsum(
        "te,de->td", key_low, w_key, preferred_element_type=jnp.float32
    )
    grad_input = grad_input + jnp.einsum(
        "te,de->td", value_low, w_value, preferred_element_type=jnp.float32
    )
    grad_tokens = (grad_input + d_first).astype(jnp.bfloat16)[None]
    vectors = jnp.stack(
        [
            jnp.sum(query_low.astype(jnp.float32), axis=0),
            jnp.sum(value_low.astype(jnp.float32), axis=0),
            jnp.sum(branch_low.astype(jnp.float32), axis=0),
            grad_gain_mid,
            grad_shift_mid,
            jnp.sum(feed_low.astype(jnp.float32), axis=0),
            grad_gain_end,
            grad_shift_end,
        ]
    )
    vector_part, up_bias_part = (
        lax.psum_scatter(
            vectors.astype(jnp.bfloat16), "shard", scatter_dimension=1, tiled=True
        ).astype(jnp.float32),
        lax.psum_scatter(
            jnp.sum(up_low.astype(jnp.float32), axis=0).astype(jnp.bfloat16),
            "shard",
            scatter_dimension=0,
            tiled=True,
        ).astype(jnp.float32),
    )
    mixer_total, up_total, down_total, vector_total, up_bias_total = (
        lax.psum(mixer_part, "rep").astype(jnp.float32),
        lax.psum(grad_up, "rep").astype(jnp.float32),
        lax.psum(grad_down, "rep").astype(jnp.float32),
        lax.psum(vector_part.astype(jnp.bfloat16), "rep").astype(jnp.float32),
        lax.psum(up_bias_part.astype(jnp.bfloat16), "rep").astype(jnp.float32),
    )
    return (
        output,
        grad_tokens,
        mixer_total[:, 0:D],
        mixer_total[:, D : 2 * D],
        mixer_total[:, 2 * D : 3 * D],
        vector_total[0],
        vector_total[1],
        mixer_total[:, 3 * D : 4 * D],
        vector_total[2],
        vector_total[3],
        vector_total[4],
        up_total,
        up_bias_total,
        down_total,
        vector_total[5],
        vector_total[6],
        vector_total[7],
    )


def solution(mesh):
    in_specs = (
        P("rep", "shard", None),
        P("rep", "shard"),
        P("rep", "shard"),
        P("shard", None),
        P("shard", None),
        P("shard", None),
        P("shard"),
        P("shard"),
        P("shard", None),
        P("shard"),
        P("shard"),
        P("shard"),
        P("shard", None),
        P("shard"),
        P("shard", None),
        P("shard"),
        P("shard"),
        P("shard"),
        P("rep", "shard", None),
    )
    out_specs = (
        P("rep", "shard", None),
        P("rep", "shard", None),
        P("shard", None),
        P("shard", None),
        P("shard", None),
        P("shard"),
        P("shard"),
        P("shard", None),
        P("shard"),
        P("shard"),
        P("shard"),
        P("shard", None),
        P("shard"),
        P("shard", None),
        P("shard"),
        P("shard"),
        P("shard"),
    )
    return jax.shard_map(shards, mesh=mesh, in_specs=in_specs, out_specs=out_specs, check_vma=False)
```

profile of v0, /device:TPU:0, one launch (start us, length us, event | category | flops | bytes accessed | tf_op | source)
XLA Modules:
  0.0 958.1 jit_solution(7064987100216604116)
XLA Ops:
  12.3 39.7 %all-gather.10.cloned.1.call-done = bf16[768,768]{1,0:T(8,128)(2,1)} async-done(((bf16[48,768]{1,0:T(8,128)(2,1)}), bf16[768,768]{1,0:T(8,128)(2,1)}) %all-gather.10.cloned.1.call-update) | async-done | bytes 1179664 | tf_op jit(solution)/shard_map/all_gather | solution.py:140
  52.0 2.5 convolution_convert_fusion.7
  58.3 59.9 %all-reduce.12 = (bf16[768]{0:T(1024)(128)(2,1)S(1)}, bf16[768]{0:T(1024)(128)(2,1)S(1)}, bf16[3072]{0:T(1024)(128)(2,1)S(1)}, bf16[768]{0:T(1024)(128)(2,1)S(1)...) all-reduce(bf16[768]{0:T(1024)(128)(2,1)S(1)} %dynamic-update-slice, ...), channel_id=1, replica_groups=mesh['rep'=2,'shard'=16] {'shard'}, use_global_device_ids=true, to_apply=%add.1 | all-reduce | flops 8448 | bytes 33792
  118.2 2.4 fusion.67
  123.5 59.3 %all-reduce = s32[3072]{0:T(1024)S(1)} all-reduce(s32[3072]{0:T(1024)S(1)} %dynamic-update-slice), channel_id=2, replica_groups=mesh['rep'=2,'shard'=16] {'shard'}, use_global_device_ids=true, to_apply=%add | all-reduce | flops 3072 | bytes 24576
  185.3 2.0 all-gather.12.cloned.1.call-done
  187.3 15.0 %reshape.236 = bf16[6,512,12,64]{3,2,1,0:T(8,128)(2,1)} reshape(bf16[3072,768]{1,0:T(8,128)(2,1)} %all-gather.12.cloned.1.call-done) | data formatting | bytes 9437184 | tf_op jit(solution)/shard_map/reshape;reshape | solution.py:23
  202.3 13.6 %copy.64 = bf16[6,512,12,64]{1,3,2,0:T(8,128)(2,1)} copy(bf16[6,512,12,64]{3,2,1,0:T(8,128)(2,1)} %reshape.236) | data formatting | bytes 9437184
  215.9 25.9 %all-gather.18.cloned.1.call-done = bf16[3072,768]{1,0:T(8,128)(2,1)} async-done(((bf16[192,768]{1,0:T(8,128)(2,1)}), bf16[3072,768]{1,0:T(8,128)(2,1)}) %all-gather.18.cloned.1.call-update) | async-done | bytes 4718608 | tf_op jit(solution)/shard_map/all_gather | solution.py:172
  241.9 15.0 %reshape.237 = bf16[6,512,12,64]{3,2,1,0:T(8,128)(2,1)} reshape(bf16[3072,768]{1,0:T(8,128)(2,1)} %all-gather.18.cloned.1.call-done) | data formatting | bytes 9437184 | tf_op jit(solution)/shard_map/reshape;reshape | solution.py:23
  256.9 13.5 %copy.65 = bf16[6,512,12,64]{1,3,2,0:T(8,128)(2,1)} copy(bf16[6,512,12,64]{3,2,1,0:T(8,128)(2,1)} %reshape.237) | data formatting | bytes 9437184
  270.4 44.5 %while.28 = (s32[]{:T(128)}, f32[12,192]{1,0:T(8,128)S(1)}, f32[12,192]{1,0:T(8,128)S(1)}, f32[192,12,64]{0,2,1:T(8,128)S(1)}, s32[192]{0:T(256)S(1)}, /*index=5...) while((s32[]{:T(128)}, f32[12,192]{1,0:T(8,128)S(1)}, ...), condition=%wide.region_3.4_spmd.clone, body=%wide.region_0.3_spmd.clone.sunk | while | flops 317879808 | bytes 17750924 | solution.py:28
  271.3 2.1 fusion.156
  275.1 2.7 fusion.160
  278.7 2.1 fusion.156
  282.5 2.7 fusion.160
  286.1 2.2 fusion.156
  289.9 2.7 fusion.160
  293.6 2.1 fusion.156
  297.3 2.7 fusion.160
  301.0 2.1 fusion.156
  304.7 2.7 fusion.160
  308.4 2.1 fusion.156
  312.2 2.7 fusion.160
  315.1 2.0 fusion.100
  317.9 18.6 %all-gather.22.cloned.1.call-done = bf16[768,3072]{1,0:T(8,128)(2,1)} async-done(((bf16[48,3072]{1,0:T(8,128)(2,1)}), bf16[768,3072]{1,0:T(8,128)(2,1)}) %all-gather.22.cloned.1.call-update) | async-done | bytes 4718608 | tf_op jit(solution)/shard_map/all_gather | solution.py:150
  336.5 8.9 fusion.49
  345.4 45.6 %all-gather.24.cloned.1.call-done = bf16[3072,768]{1,0:T(8,128)(2,1)} async-done(((bf16[192,768]{1,0:T(8,128)(2,1)}), bf16[3072,768]{1,0:T(8,128)(2,1)}) %all-gather.24.cloned.1.call-update) | async-done | bytes 4718608 | tf_op jit(solution)/shard_map/all_gather | solution.py:152
  391.0 4.0 fusion.101
  397.1 2.9 fusion.102
  400.0 2.4 multiply_reduce_fusion.1
  405.6 79.0 %while.29 = (s32[]{:T(128)}, f32[192,12,64]{0,2,1:T(8,128)S(1)}, bf16[6,512,1536]{2,1,0:T(8,128)(2,1)}, bf16[6,512,12,64]{1,3,2,0:T(8,128)(2,1)}, s32[192]{0:T(2...) while((s32[]{:T(128)}, f32[192,12,64]{0,2,1:T(8,128)S(1)}, ...), condition=%wide.region_14.15_spmd.clone, body=%wide.region_13.14_spmd.clone.sunk | while | flops 771244032 | bytes 44384276 | solution.py:35
  406.5 2.0 fusion.171
  410.3 2.9 fusion.172
  413.2 2.0 fusion.173
  419.6 2.0 fusion.171
  423.5 2.9 fusion.172
  426.4 2.0 fusion.173
  432.8 2.0 fusion.171
  436.6 2.9 fusion.172
  439.6 2.0 fusion.173
  446.0 2.0 fusion.171
  449.8 2.9 fusion.172
  452.7 2.0 fusion.173
  459.1 2.0 fusion.171
  462.9 2.9 fusion.172
  465.9 2.0 fusion.173
  472.3 2.0 fusion.171
  476.1 2.9 fusion.172
  479.0 2.0 fusion.173
  487.6 106.9 %reduce-scatter.10.cloned.1.call-done = bf16[192,1536]{1,0:T(8,128)(2,1)} async-done(((bf16[3072,1536]{1,0:T(8,128)(2,1)}), bf16[192,1536]{1,0:T(8,128)(2,1)}) %reduce-scatter.10.cloned.1.call-update) | async-done | bytes 589840 | tf_op jit(solution)/shard_map/reduce_scatter | solution.py:277
  597.6 2.5 pad_maximum_fusion
  600.1 6.6 copy.74
  608.1 3.7 convolution_convert_fusion.1
  613.3 3.7 convolution_convert_fusion
  621.5 33.9 %all-reduce.11 = (bf16[768]{0:T(1024)(128)(2,1)S(1)}, bf16[3072]{0:T(1024)(128)(2,1)S(1)}) all-reduce(bf16[768]{0:T(1024)(128)(2,1)S(1)} %dynamic-update-slice.9, bf16[3072]{0:T(1024)(128)(2,1)} %get-tuple-element.398), channel_id=1, replica_groups=mesh['rep'=2,'shard'=16] {'shard'}, use_global_device_ids=true, to_apply=%add.9 | all-reduce | flops 3840 | bytes 15360
  656.1 26.6 %reduce-scatter.16.cloned.1.call-done = bf16[48,3072]{1,0:T(8,128)(2,1)} async-done(((bf16[768,3072]{1,0:T(8,128)(2,1)}), bf16[48,3072]{1,0:T(8,128)(2,1)}) %reduce-scatter.16.cloned.1.call-update) | async-done | bytes 294928
  682.6 2.1 copy.75
  684.8 76.5 %reduce-scatter.12.cloned.1.call-done = bf16[48,3072]{1,0:T(8,128)(2,1)} async-done(((bf16[768,3072]{1,0:T(8,128)(2,1)}), bf16[48,3072]{1,0:T(8,128)(2,1)}) %reduce-scatter.12.cloned.1.call-update) | async-done | bytes 294928 | tf_op jit(solution)/shard_map/reduce_scatter | solution.py:227
  761.3 78.5 %reduce-scatter.14.cloned.1.call-done = bf16[192,768]{1,0:T(8,128)(2,1)} async-done(((bf16[3072,768]{1,0:T(8,128)(2,1)}), bf16[192,768]{1,0:T(8,128)(2,1)}) %reduce-scatter.14.cloned.1.call-update) | async-done | bytes 294928 | tf_op jit(solution)/shard_map/reduce_scatter | solution.py:217
  843.9 52.0 %reduce-scatter.18.cloned.1.call-done = bf16[48,8]{1,0:T(8,128)(2,1)} async-done(((bf16[768,8]{1,0:T(8,128)(2,1)}), bf16[48,8]{1,0:T(8,128)(2,1)}) %reduce-scatter.18.cloned.1.call-update) | async-done | bytes 784
  896.7 4.9 all-reduce.13
  902.7 41.9 %all-reduce.17.cloned.1.call-done = (bf16[48,3072]{0,1:T(8,128)(2,1)}, bf16[48,3072]{1,0:T(8,128)(2,1)}, bf16[192,768]{1,0:T(8,128)(2,1)}) async-done(((bf16[48,3072]{0,1:T(8,128)(2,1)}, bf16[48,3072]{1,0:T(8,128)(2,1)}, bf16[192,768]{1,0:T(8,128)(2,1)}), (bf16[48,3072]{0,1:T(8,128)(2,1)}, bf16[48,3072]{1,0:T(8,128)(2,1)}, bf16[192,768]{1,0:T(8,128)(2,1)})) %all-reduce.17.cloned.1.call-update) | async-done | bytes 884752 | tf_op jit(solution)/shard_map/psum | solution.py:333
  944.6 1.9 convert_element_type.245
  (378 shorter events, 94.6 us)
Async XLA Ops:
  7.2 47.4 %copy-start.42 = (u32[32]{0:T(128)S(1)}, u32[32]{0:T(128)}, u32[]{:S(2)}) copy-start(u32[32]{0:T(128)} %constant.133) | copy-start | bytes 388
  7.2 111.0 %copy-start.2 = (bf16[1,192,768]{2,1,0:T(8,128)(2,1)S(1)}, bf16[1,192,768]{2,1,0:T(8,128)(2,1)}, u32[]{:S(2)}) copy-start(bf16[1,192,768]{2,1,0:T(8,128)(2,1)} %param.23) | copy-start | bytes 884740
  7.2 49.3 %copy-start.49 = (f32[48]{0:T(128)S(1)}, f32[48]{0:T(128)}, u32[]{:S(2)}) copy-start(f32[48]{0:T(128)} %param.29) | copy-start | bytes 580
  7.2 49.3 %copy-start.50 = (f32[48]{0:T(128)S(1)}, f32[48]{0:T(128)}, u32[]{:S(2)}) copy-start(f32[48]{0:T(128)} %param.30) | copy-start | bytes 580
  7.2 49.3 %copy-start.51 = (f32[48]{0:T(128)S(1)}, f32[48]{0:T(128)}, u32[]{:S(2)}) copy-start(f32[48]{0:T(128)} %param.32) | copy-start | bytes 580
  7.2 49.3 %copy-start.52 = (f32[48]{0:T(128)S(1)}, f32[48]{0:T(128)}, u32[]{:S(2)}) copy-start(f32[48]{0:T(128)} %param.33) | copy-start | bytes 580
  7.3 49.3 %copy-start.53 = (f32[48]{0:T(128)S(1)}, f32[48]{0:T(128)}, u32[]{:S(2)}) copy-start(f32[48]{0:T(128)} %param.34) | copy-start | bytes 580
  7.3 49.3 %copy-start.48 = (f32[192]{0:T(256)S(1)}, f32[192]{0:T(256)}, u32[]{:S(2)}) copy-start(f32[192]{0:T(256)} %param.36) | copy-start | bytes 2308
  7.3 49.3 %copy-start.54 = (f32[48]{0:T(128)S(1)}, f32[48]{0:T(128)}, u32[]{:S(2)}) copy-start(f32[48]{0:T(128)} %param.38) | copy-start | bytes 580
  7.3 49.3 %copy-start.55 = (f32[48]{0:T(128)S(1)}, f32[48]{0:T(128)}, u32[]{:S(2)}) copy-start(f32[48]{0:T(128)} %param.39) | copy-start | bytes 580
  7.3 44.7 %all-gather.10.cloned.1.call-start = ((), (), s32[]{:S(2)}) async-start(), calls=%async_computation.5 | async-start | bytes 1253376 | tf_op jit(solution)/shard_map/all_gather | solution.py:140
  9.0 109.2 %all-gather.16.cloned.1.call-start = ((), (), s32[]{:S(2)}) async-start(), calls=%async_computation.8 | async-start | bytes 1253376 | tf_op jit(solution)/shard_map/all_gather | solution.py:141
  10.6 110.1 %copy-start.30 = (f32[48,768]{1,0:T(8,128)S(1)}, f32[48,768]{1,0:T(8,128)}, u32[]{:S(2)}) copy-start(f32[48,768]{1,0:T(8,128)} %param.31) | copy-start | bytes 442372
  10.6 172.8 %all-gather.14.cloned.1.call-start = ((), (), s32[]{:S(2)}) async-start(), calls=%async_computation.7 | async-start | bytes 1253376 | tf_op jit(solution)/shard_map/all_gather | solution.py:139
  12.2 109.2 %copy-start.28 = (f32[48,3072]{1,0:T(8,128)S(1)}, f32[48,3072]{1,0:T(8,128)}, u32[]{:S(2)}) copy-start(f32[48,3072]{1,0:T(8,128)} %param.35) | copy-start | bytes 1769476
  12.2 175.1 %all-gather.12.cloned.1.call-start = ((), (), s32[]{:S(2)}) async-start(), calls=%async_computation.6 | async-start | bytes 5013504 | tf_op jit(solution)/shard_map/all_gather | solution.py:171
  54.5 67.8 %copy-start.29 = (f32[192,768]{1,0:T(8,128)S(1)}, f32[192,768]{1,0:T(8,128)}, u32[]{:S(2)}) copy-start(f32[192,768]{1,0:T(8,128)} %param.37) | copy-start | bytes 1769476
  54.5 187.3 %all-gather.18.cloned.1.call-start = ((), (), s32[]{:S(2)}) async-start(), calls=%async_computation.9 | async-start | bytes 5013504 | tf_op jit(solution)/shard_map/all_gather | solution.py:172
  118.2 5.0 copy-start.45
  118.2 5.0 copy-start.46
  120.7 194.4 %all-gather.20.cloned.1.call-start = ((), (), s32[]{:S(2)}) async-start(), calls=%async_computation.10 | async-start | bytes 1253376 | tf_op jit(solution)/shard_map/all_gather | solution.py:142
  121.4 215.1 %all-gather.22.cloned.1.call-start = ((), (), s32[]{:S(2)}) async-start(), calls=%async_computation.11 | async-start | bytes 5013504 | tf_op jit(solution)/shard_map/all_gather | solution.py:150
  122.2 268.8 %all-gather.24.cloned.1.call-start = ((), (), s32[]{:S(2)}) async-start(), calls=%async_computation.12 | async-start | bytes 5013504 | tf_op jit(solution)/shard_map/all_gather | solution.py:152
  123.0 471.5 %reduce-scatter.10.cloned.1.call-start = ((), (), s32[]{:S(2)}) async-start(), calls=%async_computation.13 | async-start | bytes 10027008 | tf_op jit(solution)/shard_map/reduce_scatter | solution.py:277
  315.0 30.3 %copy-start.15 = (bf16[192,12,64]{0,2,1:T(8,128)(2,1)}, bf16[192,12,64]{0,2,1:T(8,128)(2,1)S(1)}, u32[]{:S(2)}) copy-start(bf16[192,12,64]{0,2,1:T(8,128)(2,1)S(1)} %fusion.78) | copy-start | bytes 884740
  317.0 85.4 %copy-start.4 = (f32[192,768]{1,0:T(8,128)}, f32[192,768]{1,0:T(8,128)S(1)}, u32[]{:S(2)}) copy-start(f32[192,768]{1,0:T(8,128)S(1)} %get-tuple-element.393) | copy-start | bytes 1769476
  317.0 85.4 %copy-start.31 = (f32[192]{0:T(256)}, f32[192]{0:T(256)S(1)}, u32[]{:S(2)}) copy-start(f32[192]{0:T(256)S(1)} %broadcast_multiply_fusion.5) | copy-start | bytes 2308
  317.3 85.2 %copy-start.35 = (f32[192]{0:T(256)}, f32[192]{0:T(256)S(1)}, u32[]{:S(2)}) copy-start(f32[192]{0:T(256)S(1)} %add_rsqrt_fusion.1) | copy-start | bytes 2308
  391.0 6.0 slice-start.2
  391.0 4.3 copy-start.19
  391.0 6.0 slice-start.3
  395.1 2.0 copy-start.57
  395.1 4.9 copy-start.33
  395.3 4.7 copy-start.37
  396.2 3.8 slice-start
  397.1 2.9 copy-start.21
  397.1 2.9 slice-start.1
  400.0 2.5 copy-start.26
  405.6 4.7 copy-start.24
  418.8 4.7 copy-start.24
  431.9 4.7 copy-start.24
  445.1 4.7 copy-start.24
  458.3 4.7 copy-start.24
  471.4 4.7 copy-start.24
  484.6 198.0 %reduce-scatter.16.cloned.1.call-start = ((), (), s32[]{:S(2)}) async-start(), calls=%async_computation.16 | async-start | bytes 5013504
  594.5 3.1 copy-start.10
  606.7 154.6 %reduce-scatter.12.cloned.1.call-start = ((), (), s32[]{:S(2)}) async-start(), calls=%async_computation.14 | async-start | bytes 5013504 | tf_op jit(solution)/shard_map/reduce_scatter | solution.py:227
  611.9 227.9 %reduce-scatter.14.cloned.1.call-start = ((), (), s32[]{:S(2)}) async-start(), calls=%async_computation.15 | async-start | bytes 5013504 | tf_op jit(solution)/shard_map/reduce_scatter | solution.py:217
  617.0 2.0 copy-start.39
  617.0 2.0 copy-start.44
  617.0 2.0 copy-start.41
  617.0 2.0 copy-start.40
  617.0 2.0 copy-start.43
  617.0 2.1 copy-start.14
  617.0 3.2 copy-start.11
  617.0 278.9 %reduce-scatter.18.cloned.1.call-start = ((), (), s32[]{:S(2)}) async-start(), calls=%async_computation.17 | async-start | bytes 208896
  620.1 219.8 %copy-start.7 = (f32[192,768]{1,0:T(8,128)S(1)}, f32[192,768]{1,0:T(8,128)}, u32[]{:S(2)}) copy-start(f32[192,768]{1,0:T(8,128)} %copy-done.6) | copy-start | bytes 1769476
  620.1 219.8 %copy-start.34 = (f32[192]{0:T(256)S(1)}, f32[192]{0:T(256)}, u32[]{:S(2)}) copy-start(f32[192]{0:T(256)} %copy-done.33) | copy-start | bytes 2308
  620.1 219.8 %copy-start.38 = (f32[192]{0:T(256)S(1)}, f32[192]{0:T(256)}, u32[]{:S(2)}) copy-start(f32[192]{0:T(256)} %copy-done.37) | copy-start | bytes 2308
  620.1 324.5 %all-reduce.17.cloned.1.call-start = ((), (), s32[]{:S(2)}) async-start(), calls=%async_computation.18 | async-start | bytes 2752512 | tf_op jit(solution)/shard_map/psum | solution.py:333
  621.5 219.2 %copy-start.23 = (f32[192,768]{1,0:T(8,128)S(1)}, f32[192,768]{1,0:T(8,128)}, u32[]{:S(2)}) copy-start(f32[192,768]{1,0:T(8,128)} %fusion.103) | copy-start | bytes 1769476
  839.8 2.8 copy-start.13
  840.8 55.9 %copy-start.47 = (bf16[192]{0:T(256)(128)(2,1)S(1)}, bf16[192]{0:T(256)(128)(2,1)}, u32[]{:S(2)}) copy-start(bf16[192]{0:T(256)(128)(2,1)} %dynamic-slice.11) | copy-start | bytes 1156
  944.6 3.7 copy-start.18
  (32 other events, 41.3 us)
Sparse Core Ops, SparseCore 0:
  11.0 41.0 all-gather.9
  54.9 37.3 all-gather.15
  95.1 37.1 all-gather.13
  135.0 52.2 all-gather.11
  190.0 51.7 all-gather.17
  244.6 36.8 all-gather.19
  284.3 52.0 all-gather.21
  339.3 51.6 all-gather.23
  484.7 109.7 reduce-scatter.9
  606.8 75.7 reduce-scatter.15
  686.5 74.7 reduce-scatter.11
  765.0 74.7 reduce-scatter.13
  843.3 52.5 reduce-scatter.17
  898.2 46.3 all-reduce.16
where the time goes:
time: 963 us; the launch traced here: 958 us
  waiting for transfers between devices  515 us (53%)
  blocking collectives  158 us (16%)
  matrix products  130 us (13%)
  local copies, waits for them, and re-layouts  106 us (11%)
  other arithmetic  31.2 us (3%)
  between operations  16.8 us (2%)
    unnamed x3, blocking collectives  153 us
    reduce_scatter x1, waiting for transfers between devices, shards(): lax.psum_scatter(key_value_terms.astype(jnp.bfloat16), 'shard', scatter_d...  107 us
    unnamed x16, waiting for transfers between devices  78.8 us
    reduce_scatter x1, waiting for transfers between devices, shards(): lax.psum_scatter(jnp.einsum('tf,td->fd', active_low, feed_low, preferred_...  78.5 us
    reduce_scatter x1, waiting for transfers between devices, shards(): lax.psum_scatter(jnp.einsum('td,tf->df', middle_low, up_low, preferred_el...  76.5 us
    unnamed x148, local copies, waits for them, and re-layouts  49.1 us
    all_gather x1, waiting for transfers between devices, shards(): lax.all_gather(down_weight.astype(jnp.bfloat16), 'shard', axis=0, tiled=T...  45.6 us
    psum x1, waiting for transfers between devices, shards(): lax.psum(mixer_part, 'rep').astype(jnp.float32)  41.9 us
  transfers between devices with their start and end apart: 14, of which 11 were waited for; matrix products, arithmetic and copies ran while one was open for 16% of the time, Pallas kernels for 0%

commit v1 on v0

--- a/solution.py
+++ b/solution.py
@@ -330,7 +330,7 @@
         ).astype(jnp.float32),
     )
     mixer_total, up_total, down_total, vector_total, up_bias_total = (
-        lax.psum(mixer_part, "rep").astype(jnp.float32),
+        jnp.sum(lax.all_gather(mixer_part, "rep"), axis=0).astype(jnp.float32),
         lax.psum(grad_up, "rep").astype(jnp.float32),
         lax.psum(grad_down, "rep").astype(jnp.float32),
         lax.psum(vector_part.astype(jnp.bfloat16), "rep").astype(jnp.float32),

time: 963 us -> 859 us (0.89)
  waiting for transfers between devices: 515 us -> 412 us
    reduce_scatter x1, waiting for transfers between devices: 76.5 us -> 0.01 us  [shards(): lax.psum_scatter(jnp.einsum('td,tf->df', middle_low, up_low, preferred_el...]
    reduce_scatter x0 -> x1, waiting for transfers between devices: none -> 71.5 us  [shards(): lax.psum_scatter(jnp.concatenate([jnp.einsum('td,te->de', own_tokens, que...]
    unnamed x16 -> x15, waiting for transfers between devices: 78.8 us -> 31.2 us
    psum x1, waiting for transfers between devices: 41.9 us -> 0.01 us  [shards(): lax.psum(grad_up, 'rep').astype(jnp.float32)]
    reduce_scatter x1, waiting for transfers between devices: 78.5 us -> 61.3 us  [shards(): lax.psum_scatter(jnp.einsum('tf,td->fd', active_low, feed_low, preferred_...]
    unnamed x148 -> x151, local copies, waits for them, and re-layouts: 49.1 us -> 42.9 us
  transfers between devices with their start and end apart: 14 -> 14, of which waited for: 11 -> 9; matrix products, arithmetic and copies ran while one was open for 16% -> 27% of each run, Pallas kernels for 0% -> 0%
where the time goes in v1:
time: 859 us; the launch traced here: 855 us
  waiting for transfers between devices  412 us (48%)
  blocking collectives  165 us (19%)
  matrix products  129 us (15%)
  local copies, waits for them, and re-layouts  97.2 us (11%)
  other arithmetic  33 us (4%)
  between operations  16.9 us (2%)
    unnamed x3, blocking collectives  152 us
    reduce_scatter x1, waiting for transfers between devices, shards(): lax.psum_scatter(key_value_terms.astype(jnp.bfloat16), 'shard', scatter_d...  111 us
    reduce_scatter x1, waiting for transfers between devices, shards(): lax.psum_scatter(jnp.concatenate([jnp.einsum('td,te->de', own_tokens, que...  71.5 us
    reduce_scatter x1, waiting for transfers between devices, shards(): lax.psum_scatter(jnp.einsum('tf,td->fd', active_low, feed_low, preferred_...  61.3 us
    all_gather x1, waiting for transfers between devices, shards(): lax.all_gather(down_weight.astype(jnp.bfloat16), 'shard', axis=0, tiled=T...  45.9 us
    unnamed x151, local copies, waits for them, and re-layouts  42.9 us
    all_gather x1, waiting for transfers between devices, shards(): lax.all_gather(key_weight.astype(jnp.bfloat16), 'shard', axis=0, tiled=True)  39.7 us
    unnamed x15, waiting for transfers between devices  31.2 us
  transfers between devices with their start and end apart: 14, of which 9 were waited for; matrix products, arithmetic and copies ran while one was open for 27% of the time, Pallas kernels for 0%

profile of v1, /device:TPU:0, one launch (start us, length us, event | category | flops | bytes accessed | tf_op | source)
XLA Modules:
  0.0 855.1 jit_solution(9248638300299919688)
XLA Ops:
  12.3 39.7 %all-gather.11.cloned.1.call-done = bf16[768,768]{1,0:T(8,128)(2,1)} async-done(((bf16[48,768]{1,0:T(8,128)(2,1)}), bf16[768,768]{1,0:T(8,128)(2,1)}) %all-gather.11.cloned.1.call-update) | async-done | bytes 1179664 | tf_op jit(solution)/shard_map/all_gather | solution.py:140
  52.0 2.5 convolution_convert_fusion.7
  58.3 59.9 %all-reduce.12 = (bf16[3072]{0:T(1024)(128)(2,1)S(1)}, bf16[768]{0:T(1024)(128)(2,1)S(1)}, bf16[768]{0:T(1024)(128)(2,1)S(1)}, bf16[768]{0:T(1024)(128)(2,1)S(1)...) all-reduce(bf16[3072]{0:T(1024)(128)(2,1)S(1)} %dynamic-update-slic, ...), channel_id=1, replica_groups=mesh['rep'=2,'shard'=16] {'shard'}, use_global_device_ids=true, to_apply=%add.6 | all-reduce | flops 8448 | bytes 33792
  118.2 2.4 fusion.67
  123.5 59.3 %all-reduce = s32[3072]{0:T(1024)S(1)} all-reduce(s32[3072]{0:T(1024)S(1)} %dynamic-update-slice), channel_id=2, replica_groups=mesh['rep'=2,'shard'=16] {'shard'}, use_global_device_ids=true, to_apply=%add | all-reduce | flops 3072 | bytes 24576
  184.8 2.6 all-gather.13.cloned.1.call-done
  187.3 15.1 %reshape.237 = bf16[6,512,12,64]{3,2,1,0:T(8,128)(2,1)} reshape(bf16[3072,768]{1,0:T(8,128)(2,1)} %all-gather.13.cloned.1.call-done) | data formatting | bytes 9437184 | tf_op jit(solution)/shard_map/reshape;reshape | solution.py:23
  202.4 13.5 %copy.57 = bf16[6,512,12,64]{1,3,2,0:T(8,128)(2,1)} copy(bf16[6,512,12,64]{3,2,1,0:T(8,128)(2,1)} %reshape.237) | data formatting | bytes 9437184
  215.9 25.9 %all-gather.19.cloned.1.call-done = bf16[3072,768]{1,0:T(8,128)(2,1)} async-done(((bf16[192,768]{1,0:T(8,128)(2,1)}), bf16[3072,768]{1,0:T(8,128)(2,1)}) %all-gather.19.cloned.1.call-update) | async-done | bytes 4718608 | tf_op jit(solution)/shard_map/all_gather | solution.py:172
  241.9 15.1 %reshape.238 = bf16[6,512,12,64]{3,2,1,0:T(8,128)(2,1)} reshape(bf16[3072,768]{1,0:T(8,128)(2,1)} %all-gather.19.cloned.1.call-done) | data formatting | bytes 9437184 | tf_op jit(solution)/shard_map/reshape;reshape | solution.py:23
  256.9 13.5 %copy.58 = bf16[6,512,12,64]{1,3,2,0:T(8,128)(2,1)} copy(bf16[6,512,12,64]{3,2,1,0:T(8,128)(2,1)} %reshape.238) | data formatting | bytes 9437184
  270.5 40.2 %while.28 = (s32[]{:T(128)}, f32[12,192]{1,0:T(8,128)S(1)}, f32[12,192]{1,0:T(8,128)S(1)}, f32[192,12,64]{0,2,1:T(8,128)S(1)}, s32[192]{0:T(256)S(1)}, /*index=5...) while((s32[]{:T(128)}, f32[12,192]{1,0:T(8,128)S(1)}, ...), condition=%wide.region_3.4_spmd.clone, body=%wide.region_0.3_spmd.clone.sunk | while | flops 317879808 | bytes 17750924 | solution.py:28
  270.6 2.1 fusion.156
  274.4 2.7 fusion.160
  277.3 2.2 fusion.156
  281.1 2.7 fusion.160
  284.0 2.1 fusion.156
  287.8 2.7 fusion.160
  290.7 2.2 fusion.156
  294.5 2.7 fusion.160
  297.4 2.2 fusion.156
  301.2 2.7 fusion.160
  304.2 2.1 fusion.156
  307.9 2.7 fusion.160
  313.7 22.7 %all-gather.23.cloned.1.call-done = bf16[768,3072]{1,0:T(8,128)(2,1)} async-done(((bf16[48,3072]{1,0:T(8,128)(2,1)}), bf16[768,3072]{1,0:T(8,128)(2,1)}) %all-gather.23.cloned.1.call-update) | async-done | bytes 4718608 | tf_op jit(solution)/shard_map/all_gather | solution.py:150
  336.3 8.6 %fusion.49 = (bf16[192,3072]{1,0:T(8,128)(2,1)S(1)}, f32[192,3072]{1,0:T(8,128)}) fusion(f32[3072]{0:T(1024)S(1)} %convert_element_type.218, bf16[768,3072]{1,0:T(8,128)(2,1)} %all-gather.23.cloned.1.call-done, f32[192,768]{1,0:T(8,128)S(1)} %get-tuple-element.341, f32[768]{0:T(1024)S(1)} %convert_element_type.214, f32[768]{0:T(1024)S(1)} %convert_element_type.212, ...), kind=kOutput, calls=%fused_computation.66 | convolution fusion | flops 945635328 | bytes 8867328 | tf_op jit(solution)/shard_map/dot_general | solution.py:201
  345.0 45.9 %all-gather.25.cloned.1.call-done = bf16[3072,768]{1,0:T(8,128)(2,1)} async-done(((bf16[192,768]{1,0:T(8,128)(2,1)}), bf16[3072,768]{1,0:T(8,128)(2,1)}) %all-gather.25.cloned.1.call-update) | async-done | bytes 4718608 | tf_op jit(solution)/shard_map/all_gather | solution.py:152
  390.9 3.7 fusion.101
  397.3 2.9 fusion.102
  401.3 3.7 convolution_convert_fusion.1
  405.1 5.2 multiply_reduce_fusion.1
  415.8 3.7 convolution_convert_fusion
  420.1 75.1 %while.29 = (s32[]{:T(128)}, f32[192,12,64]{0,2,1:T(8,128)S(1)}, bf16[6,512,1536]{2,1,0:T(8,128)(2,1)}, bf16[6,512,12,64]{1,3,2,0:T(8,128)(2,1)}, s32[192]{0:T(2...) while((s32[]{:T(128)}, f32[192,12,64]{0,2,1:T(8,128)S(1)}, ...), condition=%wide.region_14.15_spmd.clone, body=%wide.region_13.14_spmd.clone.sunk | while | flops 771244032 | bytes 44517508 | solution.py:35
  420.9 2.0 fusion.171
  424.1 2.9 fusion.172
  427.0 2.0 fusion.173
  433.5 2.0 fusion.171
  436.6 2.9 fusion.172
  439.5 2.1 fusion.173
  446.0 2.0 fusion.171
  449.1 2.9 fusion.172
  452.1 2.0 fusion.173
  458.5 2.0 fusion.171
  461.6 2.9 fusion.172
  464.5 2.0 fusion.173
  471.0 2.0 fusion.171
  474.1 2.9 fusion.172
  477.0 2.0 fusion.173
  483.4 2.0 fusion.171
  486.6 2.9 fusion.172
  489.5 2.1 fusion.173
  496.6 61.3 %reduce-scatter.14.cloned.1.call-done = bf16[192,768]{1,0:T(8,128)(2,1)} async-done(((bf16[3072,768]{1,0:T(8,128)(2,1)}), bf16[192,768]{1,0:T(8,128)(2,1)}) %reduce-scatter.14.cloned.1.call-update) | async-done | bytes 294928 | tf_op jit(solution)/shard_map/reduce_scatter | solution.py:217
  558.5 2.5 convolution_convert_fusion.2
  561.0 111.5 %reduce-scatter.10.cloned.1.call-done = bf16[192,1536]{1,0:T(8,128)(2,1)} async-done(((bf16[3072,1536]{1,0:T(8,128)(2,1)}), bf16[192,1536]{1,0:T(8,128)(2,1)}) %reduce-scatter.10.cloned.1.call-update) | async-done | bytes 589840 | tf_op jit(solution)/shard_map/reduce_scatter | solution.py:277
  676.9 2.5 pad_maximum_fusion
  679.4 6.6 copy.64
  687.6 32.6 %all-reduce.11 = (bf16[768]{0:T(1024)(128)(2,1)S(1)}, bf16[3072]{0:T(1024)(128)(2,1)S(1)}) all-reduce(bf16[768]{0:T(1024)(128)(2,1)S(1)} %dynamic-update-slice.9, bf16[3072]{0:T(1024)(128)(2,1)S(1)} %copy-done.52), channel_id=1, replica_groups=mesh['rep'=2,'shard'=16] {'shard'}, use_global_device_ids=true, to_apply=%add.9 | all-reduce | flops 3840 | bytes 15360
  721.2 2.5 fusion.103
  723.7 1.9 convert_element_type.247
  725.7 1.8 convert_element_type.250
  730.4 31.0 %reduce-scatter.18.cloned.1.call-done = bf16[48,8]{1,0:T(8,128)(2,1)} async-done(((bf16[768,8]{1,0:T(8,128)(2,1)}), bf16[48,8]{1,0:T(8,128)(2,1)}) %reduce-scatter.18.cloned.1.call-update) | async-done | bytes 784
  762.1 4.9 all-reduce.13
  768.1 71.5 %reduce-scatter.16.cloned.1.call-done = bf16[48,3072]{1,0:T(8,128)(2,1)} async-done(((bf16[768,3072]{1,0:T(8,128)(2,1)}), bf16[48,3072]{1,0:T(8,128)(2,1)}) %reduce-scatter.16.cloned.1.call-update) | async-done | bytes 294928 | tf_op jit(solution)/shard_map/reduce_scatter | solution.py:285
  839.6 7.9 all-gather.1
  (430 shorter events, 81.6 us)
Async XLA Ops:
  7.2 47.4 %copy-start.53 = (u32[32]{0:T(128)S(1)}, u32[32]{0:T(128)}, u32[]{:S(2)}) copy-start(u32[32]{0:T(128)} %constant.134) | copy-start | bytes 388
  7.2 111.0 %copy-start.2 = (bf16[1,192,768]{2,1,0:T(8,128)(2,1)S(1)}, bf16[1,192,768]{2,1,0:T(8,128)(2,1)}, u32[]{:S(2)}) copy-start(bf16[1,192,768]{2,1,0:T(8,128)(2,1)} %param.23) | copy-start | bytes 884740
  7.2 49.3 %copy-start.59 = (f32[48]{0:T(128)S(1)}, f32[48]{0:T(128)}, u32[]{:S(2)}) copy-start(f32[48]{0:T(128)} %param.29) | copy-start | bytes 580
  7.2 49.3 %copy-start.60 = (f32[48]{0:T(128)S(1)}, f32[48]{0:T(128)}, u32[]{:S(2)}) copy-start(f32[48]{0:T(128)} %param.30) | copy-start | bytes 580
  7.2 49.3 %copy-start.61 = (f32[48]{0:T(128)S(1)}, f32[48]{0:T(128)}, u32[]{:S(2)}) copy-start(f32[48]{0:T(128)} %param.32) | copy-start | bytes 580
  7.2 49.3 %copy-start.62 = (f32[48]{0:T(128)S(1)}, f32[48]{0:T(128)}, u32[]{:S(2)}) copy-start(f32[48]{0:T(128)} %param.33) | copy-start | bytes 580
  7.3 49.3 %copy-start.63 = (f32[48]{0:T(128)S(1)}, f32[48]{0:T(128)}, u32[]{:S(2)}) copy-start(f32[48]{0:T(128)} %param.34) | copy-start | bytes 580
  7.3 49.3 %copy-start.58 = (f32[192]{0:T(256)S(1)}, f32[192]{0:T(256)}, u32[]{:S(2)}) copy-start(f32[192]{0:T(256)} %param.36) | copy-start | bytes 2308
  7.3 49.3 %copy-start.64 = (f32[48]{0:T(128)S(1)}, f32[48]{0:T(128)}, u32[]{:S(2)}) copy-start(f32[48]{0:T(128)} %param.38) | copy-start | bytes 580
  7.3 49.3 %copy-start.65 = (f32[48]{0:T(128)S(1)}, f32[48]{0:T(128)}, u32[]{:S(2)}) copy-start(f32[48]{0:T(128)} %param.39) | copy-start | bytes 580
  7.3 44.7 %all-gather.11.cloned.1.call-start = ((), (), s32[]{:S(2)}) async-start(), calls=%async_computation.5 | async-start | bytes 1253376 | tf_op jit(solution)/shard_map/all_gather | solution.py:140
  9.0 109.2 %all-gather.17.cloned.1.call-start = ((), (), s32[]{:S(2)}) async-start(), calls=%async_computation.8 | async-start | bytes 1253376 | tf_op jit(solution)/shard_map/all_gather | solution.py:141
  10.6 110.1 %copy-start.31 = (f32[48,768]{1,0:T(8,128)S(1)}, f32[48,768]{1,0:T(8,128)}, u32[]{:S(2)}) copy-start(f32[48,768]{1,0:T(8,128)} %param.31) | copy-start | bytes 442372
  10.6 172.2 %all-gather.15.cloned.1.call-start = ((), (), s32[]{:S(2)}) async-start(), calls=%async_computation.7 | async-start | bytes 1253376 | tf_op jit(solution)/shard_map/all_gather | solution.py:139
  12.2 109.2 %copy-start.24 = (f32[48,3072]{1,0:T(8,128)S(1)}, f32[48,3072]{1,0:T(8,128)}, u32[]{:S(2)}) copy-start(f32[48,3072]{1,0:T(8,128)} %param.35) | copy-start | bytes 1769476
  12.2 175.1 %all-gather.13.cloned.1.call-start = ((), (), s32[]{:S(2)}) async-start(), calls=%async_computation.6 | async-start | bytes 5013504 | tf_op jit(solution)/shard_map/all_gather | solution.py:171
  54.5 67.8 %copy-start.25 = (f32[192,768]{1,0:T(8,128)S(1)}, f32[192,768]{1,0:T(8,128)}, u32[]{:S(2)}) copy-start(f32[192,768]{1,0:T(8,128)} %param.37) | copy-start | bytes 1769476
  54.5 187.3 %all-gather.19.cloned.1.call-start = ((), (), s32[]{:S(2)}) async-start(), calls=%async_computation.9 | async-start | bytes 5013504 | tf_op jit(solution)/shard_map/all_gather | solution.py:172
  118.2 5.0 copy-start.56
  118.2 5.0 copy-start.57
  120.7 190.8 %all-gather.21.cloned.1.call-start = ((), (), s32[]{:S(2)}) async-start(), calls=%async_computation.10 | async-start | bytes 1253376 | tf_op jit(solution)/shard_map/all_gather | solution.py:142
  121.4 215.0 %all-gather.23.cloned.1.call-start = ((), (), s32[]{:S(2)}) async-start(), calls=%async_computation.11 | async-start | bytes 5013504 | tf_op jit(solution)/shard_map/all_gather | solution.py:150
  122.2 268.7 %all-gather.25.cloned.1.call-start = ((), (), s32[]{:S(2)}) async-start(), calls=%async_computation.12 | async-start | bytes 5013504 | tf_op jit(solution)/shard_map/all_gather | solution.py:152
  123.0 373.6 %reduce-scatter.12.cloned.1.call-start = ((), (), s32[]{:S(2)}) async-start(), calls=%async_computation.14 | async-start | bytes 5013504 | tf_op jit(solution)/shard_map/reduce_scatter | solution.py:227
  123.1 267.8 %copy-start.26 = (f32[768]{0:T(1024)}, f32[768]{0:T(1024)S(1)}, u32[]{:S(2)}) copy-start(f32[768]{0:T(1024)S(1)} %convert_element_type.212) | copy-start | bytes 9220
  123.1 267.8 %copy-start.32 = (f32[768]{0:T(1024)}, f32[768]{0:T(1024)S(1)}, u32[]{:S(2)}) copy-start(f32[768]{0:T(1024)S(1)} %convert_element_type.214) | copy-start | bytes 9220
  123.2 271.7 %copy-start.35 = (f32[768]{0:T(1024)}, f32[768]{0:T(1024)S(1)}, u32[]{:S(2)}) copy-start(f32[768]{0:T(1024)S(1)} %convert_element_type.224) | copy-start | bytes 9220
  311.4 33.6 %copy-start.15 = (bf16[192,12,64]{0,2,1:T(8,128)(2,1)}, bf16[192,12,64]{0,2,1:T(8,128)(2,1)S(1)}, u32[]{:S(2)}) copy-start(bf16[192,12,64]{0,2,1:T(8,128)(2,1)S(1)} %fusion.78) | copy-start | bytes 884740
  313.4 86.8 %copy-start.37 = (f32[192]{0:T(256)}, f32[192]{0:T(256)S(1)}, u32[]{:S(2)}) copy-start(f32[192]{0:T(256)S(1)} %broadcast_multiply_fusion.5) | copy-start | bytes 2308
  313.7 86.6 %copy-start.43 = (f32[192]{0:T(256)}, f32[192]{0:T(256)S(1)}, u32[]{:S(2)}) copy-start(f32[192]{0:T(256)S(1)} %add_rsqrt_fusion.1) | copy-start | bytes 2308
  390.9 6.4 slice-start
  390.9 6.4 slice-start.1
  394.6 5.6 copy-start.4
  394.7 5.6 copy-start.39
  394.9 5.3 copy-start.47
  405.0 152.9 %reduce-scatter.14.cloned.1.call-start = ((), (), s32[]{:S(2)}) async-start(), calls=%async_computation.15 | async-start | bytes 5013504 | tf_op jit(solution)/shard_map/reduce_scatter | solution.py:217
  405.1 5.2 copy-start.28
  405.1 5.2 copy-start.38
  405.1 5.2 copy-start.44
  411.2 4.6 copy-start.23
  419.5 253.0 %reduce-scatter.10.cloned.1.call-start = ((), (), s32[]{:S(2)}) async-start(), calls=%async_computation.13 | async-start | bytes 10027008 | tf_op jit(solution)/shard_map/reduce_scatter | solution.py:277
  432.5 4.1 copy-start.19
  432.5 4.1 copy-start.41
  432.5 4.1 copy-start.45
  445.0 4.0 copy-start.41
  445.0 4.0 copy-start.45
  457.6 4.0 copy-start.41
  457.6 4.0 copy-start.45
  470.0 4.0 copy-start.41
  470.0 4.0 copy-start.45
  482.5 4.0 copy-start.45
  495.2 62.7 %copy-start.3 = (bf16[1,192,768]{2,1,0:T(8,128)(2,1)S(1)}, bf16[1,192,768]{2,1,0:T(8,128)(2,1)}, u32[]{:S(2)}) copy-start(bf16[1,192,768]{2,1,0:T(8,128)(2,1)} %param.23) | copy-start | bytes 884740
  495.3 63.2 %copy-start.7 = (f32[192,768]{1,0:T(8,128)S(1)}, f32[192,768]{1,0:T(8,128)}, u32[]{:S(2)}) copy-start(f32[192,768]{1,0:T(8,128)} %copy-done.6) | copy-start | bytes 1769476
  495.3 228.5 %all-reduce.17.cloned.1.call-start = ((), (), s32[]{:S(2)}) async-start(), calls=%async_computation.18 | async-start | bytes 1179648 | tf_op jit(solution)/shard_map/psum | solution.py:334
  496.5 64.5 %copy-start.14 = (bf16[192,12,64]{0,2,1:T(8,128)(2,1)}, bf16[192,12,64]{0,2,1:T(8,128)(2,1)S(1)}, u32[]{:S(2)}) copy-start(bf16[192,12,64]{0,2,1:T(8,128)(2,1)S(1)} %get-tuple-element.323) | copy-start | bytes 884740
  557.9 203.4 %reduce-scatter.18.cloned.1.call-start = ((), (), s32[]{:S(2)}) async-start(), calls=%async_computation.17 | async-start | bytes 208896
  674.5 165.2 %reduce-scatter.16.cloned.1.call-start = ((), (), s32[]{:S(2)}) async-start(), calls=%async_computation.16 | async-start | bytes 5013504 | tf_op jit(solution)/shard_map/reduce_scatter | solution.py:285
  686.1 34.2 %copy-start.5 = (f32[192,768]{1,0:T(8,128)S(1)}, f32[192,768]{1,0:T(8,128)}, u32[]{:S(2)}) copy-start(f32[192,768]{1,0:T(8,128)} %copy-done.4) | copy-start | bytes 1769476
  686.1 34.2 %copy-start.36 = (f32[768]{0:T(1024)S(1)}, f32[768]{0:T(1024)}, u32[]{:S(2)}) copy-start(f32[768]{0:T(1024)} %copy-done.35) | copy-start | bytes 9220
  686.1 34.2 %copy-start.40 = (f32[192]{0:T(256)S(1)}, f32[192]{0:T(256)}, u32[]{:S(2)}) copy-start(f32[192]{0:T(256)} %copy-done.39) | copy-start | bytes 2308
  686.1 34.2 %copy-start.48 = (f32[192]{0:T(256)S(1)}, f32[192]{0:T(256)}, u32[]{:S(2)}) copy-start(f32[192]{0:T(256)} %copy-done.47) | copy-start | bytes 2308
  686.1 35.1 %copy-start.9 = (bf16[768,768]{1,0:T(8,128)(2,1)S(1)}, bf16[768,768]{1,0:T(8,128)(2,1)}, u32[]{:S(2)}) copy-start(bf16[768,768]{1,0:T(8,128)(2,1)} %all-gather.15.cloned.1.call-done) | copy-start | bytes 3538948
  721.2 6.2 copy-start.11
  723.7 5.4 copy-start.12
  (60 other events, 114.7 us)
Sparse Core Ops, SparseCore 0:
  11.0 41.0 all-gather.10
  54.9 37.3 all-gather.16
  95.1 37.1 all-gather.14
  135.0 52.2 all-gather.12
  190.0 51.8 all-gather.18
  244.6 36.8 all-gather.20
  284.3 51.9 all-gather.22
  339.2 51.6 all-gather.24
  405.2 74.1 reduce-scatter.11
  483.0 74.8 reduce-scatter.13
  562.0 110.4 reduce-scatter.9
  674.7 29.6 all-reduce.16
  707.9 53.3 reduce-scatter.17
  765.0 74.5 reduce-scatter.15
